TPU v7x, 32 devices: a whole 2x2x4 slice. The times are simulated.
32 devices in a mesh: grp: 4 (over z), mem: 8 (over y, x, core).
Axes of the slice: x: 2, y: 2, z: 4, core: 2. Of those that a mesh axis runs over, the one named last changes fastest.
Arguments:
- embeddings: bfloat16 [32768, 4096], P(('grp', 'mem')), may hold values from -6 to 6
- local_picks: int32 [4, 64], P('grp', 'mem'), may hold values from 0 to 1023
- second_picks: int32 [4, 16], P('grp'), may hold values from 0 to 63
- final_picks: int32 [16], replicated, may hold values from 0 to 63
Outputs:
- gain_table: float32 [64, 64], P('grp', 'mem')
- final_cover: float32 [32768], P(('grp', 'mem'))
Inputs may be any that keep to these rules, and one draw needn't show every extreme that they name: `local_picks`: entry (g, m * 8 + k) names a row among the 1024 points of device m of group g; repeats may occur. `second_picks`: candidate indices of the group, in greedy order; repeats may occur. `final_picks`: index g * 16 + t names group g's second-round pick t; repeats may occur.
All inputs are finite; a program needn't handle non-finite values.
Results may differ from a plain program's by a relative error of at most 0.0003.
Values may be sent and summed in bfloat16 or wider, within the bound.
A program may use at most 64 MiB of HBM per device.

v0:
```python
import jax
import jax.numpy as jnp
from jax import lax
from jax.sharding import PartitionSpec as P

D = 4096


def per_device(embeddings, local_picks, second_picks, final_picks):
    scaling = float(D) ** (-0.5)
    point_count = embeddings.shape[0]
    local_count = local_picks.shape[1]
    second_list = second_picks[0]
    member = lax.axis_index("mem")
    choose = (local_picks[0][:, None] == lax.iota(jnp.int32, point_count)[None, :]).astype(
        jnp.bfloat16
    )
    own_rows = jnp.dot(choose, embeddings, preferred_element_type=jnp.float32).astype(jnp.bfloat16)

    def similar(other_rows):
        dims = (((1,), (1,)), ((), ()))
        return (
            lax.dot_general(embeddings, other_rows, dims, preferred_element_type=jnp.float32)
            * scaling
        )

    candidates = lax.all_gather(own_rows, "mem", axis=0, tiled=True)
    similar_map = similar(candidates)
    cand_total = candidates.shape[0]
    pick_table = (second_list[:, None] == lax.iota(jnp.int32, cand_total)[None, :]).astype(
        jnp.bfloat16
    )
    winners = jnp.dot(pick_table, candidates, preferred_element_type=jnp.float32).astype(
        jnp.bfloat16
    )
    union_rows = lax.all_gather(winners, "grp", axis=0, tiled=True)
    final_table = (
        final_picks[:, None] == lax.iota(jnp.int32, union_rows.shape[0])[None, :]
    ).astype(jnp.bfloat16)
    final_rows = jnp.dot(final_table, union_rows, preferred_element_type=jnp.float32).astype(
        jnp.bfloat16
    )
    own_block = lax.dynamic_slice_in_dim(similar_map, member * local_count, local_count, 1)
    coverage = jnp.max(own_block, axis=1)
    chosen_cols = jnp.take(similar_map, second_list, axis=1)

    def greedy_step(cover_now, column):
        partial_value = jnp.sum(jnp.maximum(similar_map - cover_now[:, None], 0.0), axis=0)
        return (jnp.maximum(cover_now, column), partial_value)

    _, partials = lax.scan(greedy_step, coverage, chosen_cols.T)
    gain_table = lax.psum_scatter(partials, "mem", scatter_dimension=1, tiled=True) / point_count
    final_cover = jnp.max(similar(final_rows), axis=1)
    return (gain_table, final_cover)


def solution(mesh):
    placed = (P(("grp", "mem"), None), P("grp", "mem"), P("grp", None), P())
    return jax.shard_map(
        per_device,
        mesh=mesh,
        in_specs=placed,
        out_specs=(P("grp", "mem"), P(("grp", "mem"))),
        check_vma=False,
    )
```

profile of v0, /device:TPU:0, one launch (start us, length us, event | category | flops | bytes accessed | tf_op | source)
XLA Modules:
  0.0 75.5 jit_solution(6943562138550951512)
XLA Ops:
  0.6 0.0 copy-start.2
  0.6 1.2 %dynamic-slice.4 = u32[1]{0:T(128)} dynamic-slice(u32[32]{0:T(128)} %constant.50, u32[]{:T(128)S(6)} %add.27), dynamic_slice_sizes={1} | dynamic-slice | bytes 12
  2.5 0.7 compare_and_fusion
  3.2 0.7 fusion.7
  3.9 0.0 copy-start
  3.9 4.8 %convolution_convert_fusion.2 = bf16[8,4096]{1,0:T(8,128)(2,1)S(1)} fusion(bf16[1024,4096]{1,0:T(8,128)(2,1)} %param.6, s32[8]{0:T(128)} %bitcast.25), kind=kOutput, calls=%fused_computation.5 | convolution fusion | flops 67149824 | bytes 8454176 | tf_op jit(solution)/shard_map/dot_general | solution.py:18
  8.7 11.3 %all_gather.6 = bf16[64,4096]{1,0:T(8,128)(2,1)S(1)} all-gather(bf16[8,4096]{1,0:T(8,128)(2,1)S(1)} %convolution_convert_fusion.2), channel_id=1, replica_groups=mesh['grp'=4,'mem'=8] {'mem'}, dimensions={0}, use_global_device_ids=true | all-gather | bytes 589824 | tf_op jit(solution)/shard_map/all_gather | solution.py:27
  20.0 0.0 copy-done.2
  20.0 0.2 convolution_convert_fusion.1
  20.2 0.0 copy-done
  20.3 0.0 copy-start.1
  20.3 2.7 %convolution_multiply_fusion = f32[64,1024]{1,0:T(8,128)S(1)} fusion(bf16[64,4096]{1,0:T(8,128)(2,1)S(1)} %all_gather.6, bf16[1024,4096]{1,0:T(8,128)(2,1)S(1)} %copy-done), kind=kOutput, calls=%fused_computation.6 | convolution fusion | flops 536936448 | bytes 9175040 | tf_op jit(solution)/shard_map/dot_general | solution.py:23
  23.0 0.6 gather_fusion
  23.5 0.1 broadcast_select_fusion
  23.6 0.2 copy.8
  23.8 4.8 %while.12 = (s32[]{:T(128)}, f32[1024]{0:T(1024)S(1)}, f32[16,64]{1,0:T(8,128)S(1)}, f32[16,1024]{1,0:T(8,128)S(1)}, f32[1024,64]{1,0:T(8,128)S(1)}, /*index=5*/s32[]{:T(128)}, s32[]{:T(128)}) while((s32[]{:T(128)}, f32[1024]{0:T(1024)S(1)}, f32[16,64]{1,0:T(8,128)S(1)}, f32[16,1024]{1,0:T(8,128)S(1)}, f32[1024,64]{1,0:T(8,128)S(1)}, ...), condition=%wide.region_3.4_spmd, body=%wide.region_1.0_spmd.sunk | while | flops 197570 | bytes 287581 | solution.py:51
  23.8 0.2 maximum_reduce_fusion.2
  24.1 0.2 maximum_reduce_fusion.2
  24.4 0.2 maximum_reduce_fusion.2
  24.7 0.2 maximum_reduce_fusion.2
  25.0 0.2 maximum_reduce_fusion.2
  25.3 0.2 maximum_reduce_fusion.2
  25.6 0.2 maximum_reduce_fusion.2
  25.9 0.2 maximum_reduce_fusion.2
  26.2 0.2 maximum_reduce_fusion.2
  26.5 0.2 maximum_reduce_fusion.2
  26.8 0.2 maximum_reduce_fusion.2
  27.1 0.2 maximum_reduce_fusion.2
  27.5 0.2 maximum_reduce_fusion.2
  27.8 0.2 maximum_reduce_fusion.2
  28.1 0.2 maximum_reduce_fusion.2
  28.4 0.2 maximum_reduce_fusion.2
  28.7 0.1 copy.9
  28.7 23.6 %all-reduce = f32[16,64]{0,1:T(8,128)S(1)} all-reduce(f32[16,64]{0,1:T(8,128)S(1)} %copy.9), channel_id=2, replica_groups=mesh['grp'=4,'mem'=8] {'mem'}, use_global_device_ids=true, to_apply=%region_4.5.clone | all-reduce | flops 1024 | bytes 8192
  52.3 0.6 dynamic-slice_multiply_fusion
  52.9 16.2 %all_gather.7 = bf16[64,4096]{1,0:T(8,128)(2,1)S(1)} all-gather(bf16[16,4096]{1,0:T(8,128)(2,1)S(1)} %convolution_convert_fusion.1), channel_id=1, replica_groups=mesh['grp'=4,'mem'=8] {'grp'}, dimensions={0}, use_global_device_ids=true | all-gather | bytes 655360 | tf_op jit(solution)/shard_map/all_gather | solution.py:36
  69.1 0.0 copy-done.1
  69.1 6.4 %fusion.2 = f32[1024]{0:T(1024)} fusion(bf16[1024,4096]{1,0:T(8,128)(2,1)} %param.6, bf16[64,4096]{1,0:T(8,128)(2,1)S(1)} %all_gather.7, s32[16]{0:T(128)S(1)} %copy-done.1), kind=kOutput, calls=%fused_computation.9 | convolution fusion | flops 142704640 | bytes 8917056 | tf_op jit(solution)/shard_map/dot_general | solution.py:23
  (51 shorter events, 0.9 us)
Async XLA Ops:
  0.6 19.4 %copy-start.2 = (s32[1,16]{1,0:T(1,128)S(1)}, s32[1,16]{1,0:T(1,128)}, u32[]{:S(2)}) copy-start(s32[1,16]{1,0:T(1,128)} %param.8) | copy-start | bytes 196
  3.9 16.4 %copy-start = (bf16[1024,4096]{1,0:T(8,128)(2,1)S(1)}, bf16[1024,4096]{1,0:T(8,128)(2,1)}, u32[]{:S(2)}) copy-start(bf16[1024,4096]{1,0:T(8,128)(2,1)} %param.6) | copy-start | bytes 25165828
  20.3 48.9 %copy-start.1 = (s32[16]{0:T(128)S(1)}, s32[16]{0:T(128)}, u32[]{:S(2)}) copy-start(s32[16]{0:T(128)} %param.9) | copy-start | bytes 196
where the time goes:
time: 75.8 us; the launch traced here: 75.5 us
  blocking collectives  51.1 us (67%)
  matrix products  14.1 us (19%)
  other arithmetic  5.58 us (7%)
  local copies, waits for them, and re-layouts  2.9 us (4%)
  between operations  1.36 us (2%)
    unnamed x1, blocking collectives  23.6 us
    all_gather x1, blocking collectives, per_device(): union_rows = lax.all_gather(winners, 'grp', axis=0, tiled=True)  16.2 us
    all_gather x1, blocking collectives, per_device(): candidates = lax.all_gather(own_rows, 'mem', axis=0, tiled=True)  11.3 us
    dot_general x2, matrix products, similar(): lax.dot_general(embeddings, other_rows, dims, preferred_element_type=jnp....  9.06 us
    dot_general x1, matrix products, per_device(): jnp.dot(choose, embeddings, preferred_element_type=jnp.float32)  4.78 us
    reduce_sum x16, other arithmetic, greedy_step(): jnp.sum(jnp.maximum(similar_map - cover_now[:, None], 0.0), axis=0)  3.49 us

commit v1 on v0

v1 whole, which is shorter than its diff:
```python
import functools

import jax
import jax.numpy as jnp
from jax import lax
from jax.experimental import pallas as pl
from jax.experimental.pallas import tpu as pltpu
from jax.sharding import PartitionSpec as P

MESH = pl.DeviceIdType.MESH
NT = (((1,), (1,)), ((), ()))
LOADS = 8
BLOCK = 16


def kernel(
    n_grp, n_mem, slices,
    emb_hbm, local_hbm, second_hbm, final_hbm,
    gain_ref, cover_ref,
    emb, local, second, final, own, part, cand, zbuf, zsum, fin, sim, gsend, gbuf,
    load_sem, pick_sem, part_send, part_recv, cand_send, cand_recv,
    z_send, z_recv, fin_send, fin_recv, g_send, g_recv,
):
    grp = lax.axis_index("grp")
    mem = lax.axis_index("mem")
    tiles, block, depth = emb.shape
    points = tiles * block
    k1 = own.shape[0]
    k2 = second.shape[1]
    k3 = final.shape[0]
    cands = n_mem * k1
    width = depth // slices
    scale = float(depth) ** -0.5
    every = slices == n_mem

    def owner(body):
        if every:
            body()
        else:
            pl.when(mem < slices)(body)

    def mem_peer(d):
        return lax.rem(mem + d, n_mem)

    def grp_peer(d):
        return lax.rem(grp + d, n_grp)

    barrier = pltpu.get_barrier_semaphore()
    for d in range(1, n_mem):
        pl.semaphore_signal(barrier, inc=1, device_id={"mem": mem_peer(d)}, device_id_type=MESH)
    for d in range(1, n_grp):
        pl.semaphore_signal(barrier, inc=1, device_id={"grp": grp_peer(d)}, device_id_type=MESH)

    picks = [
        pltpu.make_async_copy(src, dst, pick_sem.at[i])
        for i, (src, dst) in enumerate(((local_hbm, local), (second_hbm, second), (final_hbm, final)))
    ]
    for copy in picks:
        copy.start()
    rows = tiles // LOADS
    loads = [
        pltpu.make_async_copy(
            emb_hbm.at[pl.ds(i * rows, rows)], emb.at[pl.ds(i * rows, rows)], load_sem.at[i]
        )
        for i in range(LOADS)
    ]
    for copy in loads:
        copy.start()
    for copy in picks:
        copy.wait()

    def one_hot(values, lanes):
        line = lax.broadcasted_iota(jnp.int32, (len(values), lanes), 0)
        spot = lax.broadcasted_iota(jnp.int32, (len(values), lanes), 1)
        wanted = jnp.zeros((len(values), lanes), jnp.int32)
        for r, value in enumerate(values):
            wanted = jnp.where(line == r, value, wanted)
        return jnp.where(spot == wanted, 1.0, 0.0).astype(jnp.bfloat16)

    shift = block.bit_length() - 1
    starts = [local[0, r] >> shift for r in range(k1)]
    choose = one_hot([r * block + (local[0, r] & (block - 1)) for r in range(k1)], k1 * block)
    seconds = one_hot([second[0, t] for t in range(k2)], cands)
    finals_of = one_hot([final[j] - grp * k2 for j in range(k3)], k2)
    table = jnp.dot(finals_of, seconds, preferred_element_type=jnp.float32).astype(jnp.bfloat16)

    for copy in loads:
        copy.wait()
    step = depth // 4
    for c in range(0, depth, step):
        blocks = jnp.concatenate(
            [emb[s, :, c:c + step] for s in starts], axis=0
        )
        own[:, c:c + step] = jnp.dot(
            choose, blocks, preferred_element_type=jnp.float32
        ).astype(jnp.bfloat16)
    pl.semaphore_wait(barrier, n_mem - 1 + n_grp - 1)

    def part_copy(d):
        peer = mem_peer(d)
        return pltpu.make_async_remote_copy(
            src_ref=own.at[:, pl.ds(pl.multiple_of(lax.rem(peer, slices) * width, 128), width)],
            dst_ref=part.at[mem],
            send_sem=part_send.at[d - 1],
            recv_sem=part_recv.at[d - 1],
            device_id={"mem": peer},
            device_id_type=MESH,
        )

    parts = [part_copy(d) for d in range(1, n_mem)]
    for copy in parts:
        copy.start()
    bulks = [
        pltpu.make_async_remote_copy(
            src_ref=own,
            dst_ref=cand.at[mem],
            send_sem=cand_send.at[d - 1],
            recv_sem=cand_recv.at[d - 1],
            device_id={"mem": mem_peer(d)},
            device_id_type=MESH,
        )
        for d in range(1, n_mem)
    ]
    for copy in bulks:
        copy.start()
    my_cols = pl.ds(pl.multiple_of(lax.rem(mem, slices) * width, 128), width)
    part[mem] = own[:, my_cols]
    cand[mem] = own[...]

    for copy in parts:
        copy.wait_recv()
    share = jnp.dot(
        table, part[...].reshape(cands, width), preferred_element_type=jnp.float32
    ).astype(jnp.bfloat16)
    zbuf[grp] = share
    shares = [
        pltpu.make_async_remote_copy(
            src_ref=zbuf.at[grp],
            dst_ref=zbuf.at[grp],
            send_sem=z_send.at[d - 1],
            recv_sem=z_recv.at[d - 1],
            device_id={"grp": grp_peer(d)},
            device_id_type=MESH,
        )
        for d in range(1, n_grp)
    ]
    for copy in shares:
        copy.start()

    for copy in bulks:
        copy.wait_recv()
    every_cand = cand[...].reshape(cands, depth)
    winners = jnp.dot(seconds, every_cand, preferred_element_type=jnp.float32).astype(jnp.bfloat16)
    rhs = jnp.concatenate([every_cand, winners], axis=0)
    tile = points // 4
    part_rows = tiles // 4

    def rows_of(i):
        return emb[i * part_rows:(i + 1) * part_rows].reshape(tile, depth)

    def similar(i):
        sim[:, i * tile:(i + 1) * tile] = lax.dot_general(
            rhs, rows_of(i), NT, preferred_element_type=jnp.float32
        )

    similar(0)
    similar(1)

    for copy in shares:
        copy.wait_recv()
    total = zbuf[0].astype(jnp.float32)
    for g in range(1, n_grp):
        total = total + zbuf[g].astype(jnp.float32)
    zsum[...] = total.astype(jnp.bfloat16)
    finals = [
        pltpu.make_async_remote_copy(
            src_ref=zsum,
            dst_ref=fin.at[:, my_cols],
            send_sem=fin_send.at[d - 1],
            recv_sem=fin_recv.at[d - 1],
            device_id={"mem": mem_peer(d)},
            device_id_type=MESH,
        )
        for d in range(1, n_mem)
    ]

    def send_final():
        for copy in finals:
            copy.start()
        fin[:, my_cols] = zsum[...]

    owner(send_final)

    similar(2)
    similar(3)

    cover = jnp.max(sim[pl.ds(pl.multiple_of(mem * k1, k1), k1), :], axis=0, keepdims=True)
    lane = lax.broadcasted_iota(jnp.int32, (cands, 128), 1)
    gains = jnp.zeros((cands, 128), jnp.float32)
    for t in range(k2):
        acc = jnp.zeros((cands, 128), jnp.float32)
        for c in range(0, points, 128):
            acc = acc + jnp.maximum(sim[:cands, c:c + 128] - cover[:, c:c + 128], 0.0)
        gains = jnp.where(lane == t, jnp.sum(acc, axis=1, keepdims=True), gains)
        cover = jnp.maximum(cover, sim[cands + t:cands + t + 1, :])
    gsend[...] = gains.reshape(n_mem, k1, 128)
    gathers = [
        pltpu.make_async_remote_copy(
            src_ref=gsend.at[mem_peer(d)],
            dst_ref=gbuf.at[mem],
            send_sem=g_send.at[d - 1],
            recv_sem=g_recv.at[d - 1],
            device_id={"mem": mem_peer(d)},
            device_id_type=MESH,
        )
        for d in range(1, n_mem)
    ]
    for copy in gathers:
        copy.start()
    gbuf[mem] = gsend[mem]

    if every:
        for copy in finals:
            copy.wait_recv()
    else:
        for d in range(1, n_mem):
            pl.when(lax.rem(mem + n_mem - d, n_mem) < slices)(finals[d - 1].wait_recv)
    final_rows = fin[...]
    for i in range(4):
        best = lax.dot_general(
            final_rows, rows_of(i), NT, preferred_element_type=jnp.float32
        )
        cover_ref[:, i * tile:(i + 1) * tile] = jnp.max(best, axis=0, keepdims=True) * scale

    for copy in gathers:
        copy.wait_recv()
    total = jnp.sum(gbuf[...], axis=0) * (scale / points)
    wide = jnp.concatenate([total, jnp.zeros((128 - k1, 128), jnp.float32)], axis=0)
    gain_ref[...] = wide.T[:k2, :k1]

    for copy in parts + bulks + shares + gathers:
        copy.wait_send()

    def sent_final():
        for copy in finals:
            copy.wait_send()

    owner(sent_final)


def per_device(n_grp, n_mem, embeddings, local_picks, second_picks, final_picks):
    points, depth = embeddings.shape
    k1 = local_picks.shape[1]
    k2 = second_picks.shape[1]
    k3 = final_picks.shape[0]
    cands = n_mem * k1
    slices = min(n_mem, depth // 128)
    width = depth // slices
    half = jnp.bfloat16
    dma = pltpu.SemaphoreType.DMA
    gain, cover = pl.pallas_call(
        functools.partial(kernel, n_grp, n_mem, slices),
        out_shape=(
            jax.ShapeDtypeStruct((k2, k1), jnp.float32),
            jax.ShapeDtypeStruct((1, points), jnp.float32),
        ),
        in_specs=[pl.BlockSpec(memory_space=pl.ANY)] * 4,
        out_specs=(pl.BlockSpec(memory_space=pltpu.VMEM),) * 2,
        scratch_shapes=[
            pltpu.VMEM((points // BLOCK, BLOCK, depth), half),
            pltpu.SMEM(local_picks.shape, jnp.int32),
            pltpu.SMEM(second_picks.shape, jnp.int32),
            pltpu.SMEM(final_picks.shape, jnp.int32),
            pltpu.VMEM((k1, depth), half),
            pltpu.VMEM((n_mem, k1, width), half),
            pltpu.VMEM((n_mem, k1, depth), half),
            pltpu.VMEM((n_grp, k3, width), half),
            pltpu.VMEM((k3, width), half),
            pltpu.VMEM((k3, depth), half),
            pltpu.VMEM((cands + k2, points), jnp.float32),
            pltpu.VMEM((n_mem, k1, 128), jnp.float32),
            pltpu.VMEM((n_mem, k1, 128), jnp.float32),
            dma((LOADS,)), dma((3,)),
            dma((n_mem - 1,)), dma((n_mem - 1,)),
            dma((n_mem - 1,)), dma((n_mem - 1,)),
            dma((n_grp - 1,)), dma((n_grp - 1,)),
            dma((n_mem - 1,)), dma((n_mem - 1,)),
            dma((n_mem - 1,)), dma((n_mem - 1,)),
        ],
        compiler_params=pltpu.CompilerParams(
            collective_id=0, has_side_effects=True, vmem_limit_bytes=48 * 1024 * 1024
        ),
    )(embeddings.reshape(points // BLOCK, BLOCK, depth), local_picks, second_picks, final_picks)
    return gain, cover.reshape(points)


def solution(mesh):
    n_grp, n_mem = mesh.shape["grp"], mesh.shape["mem"]
    return jax.shard_map(
        functools.partial(per_device, n_grp, n_mem),
        mesh=mesh,
        in_specs=(P(("grp", "mem"), None), P("grp", "mem"), P("grp", None), P()),
        out_specs=(P("grp", "mem"), P(("grp", "mem"))),
        check_vma=False,
    )
```

time: 75.8 us -> 25.6 us (0.34)
  blocking collectives: 51.1 us -> 0 us
  Pallas kernels: 0 us -> 21.6 us
  matrix products: 14.1 us -> 0 us
  other arithmetic: 5.58 us -> 0 us
    all_gather x2 -> x0, blocking collectives: 27.5 us -> none  [the longest x1 16.2 us: per_device(): union_rows = lax.all_gather(winners, 'grp', axis=0, tiled=True)]
    unnamed x1 -> x0, blocking collectives: 23.6 us -> none
    pallas_call x0 -> x1, Pallas kernels: none -> 21.6 us  [per_device(): pl.pallas_call(functools.partial(kernel, n_grp, n_mem, slices), out_shape...]
    dot_general x4 -> x0, matrix products: 14.1 us -> none  [the longest x2 9.06 us: similar(): lax.dot_general(embeddings, other_rows, dims, preferred_element_type=jnp....]
    reduce_sum x16 -> x0, other arithmetic: 3.49 us -> none  [greedy_step(): jnp.sum(jnp.maximum(similar_map - cover_now[:, None], 0.0), axis=0)]
    unnamed x7 -> x8, local copies, waits for them, and re-layouts: 1.26 us -> 3.21 us
where the time goes in v1:
time: 25.6 us; the launch traced here: 25.5 us
  Pallas kernels  21.6 us (84%)
  local copies, waits for them, and re-layouts  3.21 us (13%)
  between operations  0.65 us (3%)
    pallas_call x1, Pallas kernels, per_device(): pl.pallas_call(functools.partial(kernel, n_grp, n_mem, slices), out_shape...  21.6 us
    unnamed x8, local copies, waits for them, and re-layouts  3.21 us

profile of v1, /device:TPU:0, one launch (start us, length us, event | category | flops | bytes accessed | tf_op | source)
XLA Modules:
  0.0 25.5 jit_solution(3775562164802186200)
XLA Ops:
  0.6 0.0 copy-start
  0.6 0.6 %copy-done = s32[1,8]{1,0:T(1,128)S(1)} copy-done((s32[1,8]{1,0:T(1,128)S(1)}, s32[1,8]{1,0:T(1,128)}, u32[]{:S(2)}) %copy-start) | copy-done | bytes 56
  1.3 0.0 copy-start.1
  1.3 0.7 %copy-done.1 = s32[1,16]{1,0:T(1,128)S(1)} copy-done((s32[1,16]{1,0:T(1,128)S(1)}, s32[1,16]{1,0:T(1,128)}, u32[]{:S(2)}) %copy-start.1) | copy-done | bytes 88
  1.9 0.0 copy-start.2
  1.9 0.7 %copy-done.2 = s32[16]{0:T(128)S(1)} copy-done((s32[16]{0:T(128)S(1)}, s32[16]{0:T(128)}, u32[]{:S(2)}) %copy-start.2) | copy-done | bytes 88
  2.6 21.6 %shard_map.59 = (f32[16,8]{1,0:T(8,128)S(1)}, f32[1,1024]{1,0:T(1,128)S(1)}) custom-call(bf16[64,16,4096]{2,1,0:T(8,128)(2,1)} %bitcast.3, s32[1,8]{1,0:T(1,128)S(1)} %copy-done, s32[1,16]{1,0:T(1,128)S(1)} %copy-done.1, s32[16]{0:T(128)S(1)} %copy-done.2), custom_call_target="tpu_custom_call" | custom-call | tf_op jit(solution)/shard_map/pallas_call | solution.py:261
  24.2 0.7 %copy.6 = f32[16,8]{0,1:T(8,128)} copy(f32[16,8]{1,0:T(8,128)S(1)} %get-tuple-element.6) | data formatting | bytes 1024
  24.9 0.6 %copy.8 = f32[1024]{0:T(1024)} copy(f32[1024]{0:T(1024)S(1)} %bitcast.2) | data formatting | bytes 8192
Async XLA Ops:
  0.6 0.7 %copy-start = (s32[1,8]{1,0:T(1,128)S(1)}, s32[1,8]{1,0:T(1,128)}, u32[]{:S(2)}) copy-start(s32[1,8]{1,0:T(1,128)} %local_hbm.1) | copy-start | bytes 100
  1.3 0.7 %copy-start.1 = (s32[1,16]{1,0:T(1,128)S(1)}, s32[1,16]{1,0:T(1,128)}, u32[]{:S(2)}) copy-start(s32[1,16]{1,0:T(1,128)} %second_hbm.1) | copy-start | bytes 196
  1.9 0.7 %copy-start.2 = (s32[16]{0:T(128)S(1)}, s32[16]{0:T(128)}, u32[]{:S(2)}) copy-start(s32[16]{0:T(128)} %final_hbm.1) | copy-start | bytes 196

commit v2 on v1

--- a/solution.py
+++ b/solution.py
@@ -235,8 +235,7 @@
     for copy in gathers:
         copy.wait_recv()
     total = jnp.sum(gbuf[...], axis=0) * (scale / points)
-    wide = jnp.concatenate([total, jnp.zeros((128 - k1, 128), jnp.float32)], axis=0)
-    gain_ref[...] = wide.T[:k2, :k1]
+    gain_ref[...] = total[:, :k2]
 
     for copy in parts + bulks + shares + gathers:
         copy.wait_send()
@@ -261,10 +260,10 @@
     gain, cover = pl.pallas_call(
         functools.partial(kernel, n_grp, n_mem, slices),
         out_shape=(
-            jax.ShapeDtypeStruct((k2, k1), jnp.float32),
+            jax.ShapeDtypeStruct((k1, k2), jnp.float32),
             jax.ShapeDtypeStruct((1, points), jnp.float32),
         ),
-        in_specs=[pl.BlockSpec(memory_space=pl.ANY)] * 4,
+        in_specs=[pl.BlockSpec(memory_space=pltpu.HBM)] * 4,
         out_specs=(pl.BlockSpec(memory_space=pltpu.VMEM),) * 2,
         scratch_shapes=[
             pltpu.VMEM((points // BLOCK, BLOCK, depth), half),
@@ -290,8 +289,9 @@
         compiler_params=pltpu.CompilerParams(
             collective_id=0, has_side_effects=True, vmem_limit_bytes=48 * 1024 * 1024
         ),
-    )(embeddings.reshape(points // BLOCK, BLOCK, depth), local_picks, second_picks, final_picks)
-    return gain, cover.reshape(points)
+    )(embeddings.reshape(points // BLOCK, BLOCK, depth),
+      *[pltpu.with_memory_space_constraint(x, pltpu.HBM) for x in (local_picks, second_picks, final_picks)])
+    return gain.T, cover.reshape(points)
 
 
 def solution(mesh):

time: 25.6 us -> 23.6 us (0.922)
  local copies, waits for them, and re-layouts: 3.21 us -> 1.19 us
    unnamed x8 -> x2, local copies, waits for them, and re-layouts: 3.21 us -> 1.19 us
where the time goes in v2:
time: 23.6 us; the launch traced here: 23.5 us
  Pallas kernels  21.6 us (92%)
  local copies, waits for them, and re-layouts  1.19 us (5%)
  between operations  0.64 us (3%)
    pallas_call x1, Pallas kernels, per_device(): pl.pallas_call(functools.partial(kernel, n_grp, n_mem, slices), out_shape...  21.6 us
    unnamed x2, local copies, waits for them, and re-layouts  1.19 us

profile of v2, /device:TPU:0, one launch (start us, length us, event | category | flops | bytes accessed | tf_op | source)
XLA Modules:
  0.0 23.5 jit_solution(4536827504430368417)
XLA Ops:
  0.6 21.6 %shard_map.59 = (f32[8,16]{1,0:T(8,128)S(1)}, f32[1,1024]{1,0:T(1,128)S(1)}) custom-call(bf16[64,16,4096]{2,1,0:T(8,128)(2,1)} %bitcast.5, s32[1,8]{1,0:T(1,128)} %local_hbm.1, s32[1,16]{1,0:T(1,128)} %second_hbm.1, s32[16]{0:T(128)} %final_hbm.1), custom_call_target="tpu_custom_call" | custom-call | tf_op jit(solution)/shard_map/pallas_call | solution.py:260
  22.3 0.6 %copy.8 = f32[16,8]{0,1:T(8,128)} copy(f32[16,8]{0,1:T(8,128)S(1)} %bitcast.4) | data formatting | bytes 1024
  22.9 0.6 %copy.9 = f32[1024]{0:T(1024)} copy(f32[1024]{0:T(1024)S(1)} %bitcast.3) | data formatting | bytes 8192

commit v3 on v2

--- a/solution.py
+++ b/solution.py
@@ -11,6 +11,7 @@
 NT = (((1,), (1,)), ((), ()))
 LOADS = 8
 BLOCK = 16
+PIECES = 2
 
 
 def kernel(
@@ -39,17 +40,25 @@
         else:
             pl.when(mem < slices)(body)
 
-    def mem_peer(d):
-        return lax.rem(mem + d, n_mem)
-
-    def grp_peer(d):
-        return lax.rem(grp + d, n_grp)
+    def peer_of(own_place, count, d):
+        peer = own_place
+        for bit in (1 << k for k in range(count.bit_length() - 1)):
+            if d & bit:
+                peer = peer + bit - 2 * bit * ((own_place // bit) % 2)
+        return peer
+
+    mem_far = range(n_mem - 1, 0, -1)
+    mem_near = range(1, n_mem)
+    across = range(2, n_mem, 2)
+    grp_far = range(n_grp - 1, 0, -1)
+    mem_peers = {d: peer_of(mem, n_mem, d) for d in mem_far}
+    grp_peers = {d: peer_of(grp, n_grp, d) for d in grp_far}
 
     barrier = pltpu.get_barrier_semaphore()
-    for d in range(1, n_mem):
-        pl.semaphore_signal(barrier, inc=1, device_id={"mem": mem_peer(d)}, device_id_type=MESH)
-    for d in range(1, n_grp):
-        pl.semaphore_signal(barrier, inc=1, device_id={"grp": grp_peer(d)}, device_id_type=MESH)
+    for d in mem_far:
+        pl.semaphore_signal(barrier, inc=1, device_id={"mem": mem_peers[d]}, device_id_type=MESH)
+    for d in grp_far:
+        pl.semaphore_signal(barrier, inc=1, device_id={"grp": grp_peers[d]}, device_id_type=MESH)
 
     picks = [
         pltpu.make_async_copy(src, dst, pick_sem.at[i])
@@ -97,7 +106,7 @@
     pl.semaphore_wait(barrier, n_mem - 1 + n_grp - 1)
 
     def part_copy(d):
-        peer = mem_peer(d)
+        peer = mem_peers[d]
         return pltpu.make_async_remote_copy(
             src_ref=own.at[:, pl.ds(pl.multiple_of(lax.rem(peer, slices) * width, 128), width)],
             dst_ref=part.at[mem],
@@ -107,25 +116,40 @@
             device_id_type=MESH,
         )
 
-    parts = [part_copy(d) for d in range(1, n_mem)]
+    parts = [part_copy(d) for d in mem_near]
     for copy in parts:
         copy.start()
-    bulks = [
-        pltpu.make_async_remote_copy(
-            src_ref=own,
-            dst_ref=cand.at[mem],
-            send_sem=cand_send.at[d - 1],
-            recv_sem=cand_recv.at[d - 1],
-            device_id={"mem": mem_peer(d)},
-            device_id_type=MESH,
-        )
-        for d in range(1, n_mem)
-    ]
-    for copy in bulks:
-        copy.start()
+    chunks, piece = cand.shape[0], cand.shape[3]
+
+    chunks, piece = cand.shape[0], cand.shape[3]
+
+    def bulk_copy(c, d, source, at, to):
+        return pltpu.make_async_remote_copy(
+            src_ref=source,
+            dst_ref=cand.at[c, at],
+            send_sem=cand_send.at[c, d - 1],
+            recv_sem=cand_recv.at[c, d - 1],
+            device_id={"mem": to},
+            device_id_type=MESH,
+        )
+
+    bulks, relays = [], []
+    for c in range(chunks):
+        mine = own.at[:, c * piece:(c + 1) * piece]
+        bulks.append([bulk_copy(c, d, mine, mem, mem_peers[d]) for d in across])
+        relays.append([bulk_copy(c, 1, mine, mem, mem_peers[1])] + [
+            bulk_copy(c, d + 1, cand.at[c, mem_peers[d]], mem_peers[d], mem_peers[1])
+            for d in across
+        ])
+    for chunk in bulks:
+        for copy in chunk:
+            copy.start()
+    for chunk in relays:
+        chunk[0].start()
     my_cols = pl.ds(pl.multiple_of(lax.rem(mem, slices) * width, 128), width)
     part[mem] = own[:, my_cols]
-    cand[mem] = own[...]
+    for c in range(chunks):
+        cand[c, mem] = own[:, c * piece:(c + 1) * piece]
 
     for copy in parts:
         copy.wait_recv()
@@ -139,32 +163,60 @@
             dst_ref=zbuf.at[grp],
             send_sem=z_send.at[d - 1],
             recv_sem=z_recv.at[d - 1],
-            device_id={"grp": grp_peer(d)},
-            device_id_type=MESH,
-        )
-        for d in range(1, n_grp)
+            device_id={"grp": grp_peers[d]},
+            device_id_type=MESH,
+        )
+        for d in grp_far
     ]
     for copy in shares:
         copy.start()
 
-    for copy in bulks:
-        copy.wait_recv()
-    every_cand = cand[...].reshape(cands, depth)
-    winners = jnp.dot(seconds, every_cand, preferred_element_type=jnp.float32).astype(jnp.bfloat16)
-    rhs = jnp.concatenate([every_cand, winners], axis=0)
-    tile = points // 4
-    part_rows = tiles // 4
-
-    def rows_of(i):
-        return emb[i * part_rows:(i + 1) * part_rows].reshape(tile, depth)
-
-    def similar(i):
-        sim[:, i * tile:(i + 1) * tile] = lax.dot_general(
-            rhs, rows_of(i), NT, preferred_element_type=jnp.float32
-        )
-
-    similar(0)
-    similar(1)
+    def relay(c):
+        for copy, onward in zip(bulks[c], relays[c][1:]):
+            copy.wait_recv()
+            onward.start()
+
+    relay(0)
+    for c in range(chunks):
+        if c + 1 < chunks:
+            relay(c + 1)
+        for copy in relays[c]:
+            copy.wait_recv()
+        every_cand = cand[c].reshape(cands, piece)
+        winners = jnp.dot(
+            seconds, every_cand, preferred_element_type=jnp.float32
+        ).astype(jnp.bfloat16)
+        rhs = jnp.concatenate([every_cand, winners], axis=0)
+        partial = lax.dot_general(
+            rhs, emb[:, :, c * piece:(c + 1) * piece].reshape(points, piece), NT,
+            preferred_element_type=jnp.float32,
+        )
+        sim[...] = partial if c == 0 else sim[...] + partial
+
+    cover = jnp.max(sim[pl.ds(pl.multiple_of(mem * k1, k1), k1), :], axis=0, keepdims=True)
+    lane = lax.broadcasted_iota(jnp.int32, (cands, 128), 1)
+    gains = jnp.zeros((cands, 128), jnp.float32)
+    for t in range(k2):
+        acc = jnp.zeros((cands, 128), jnp.float32)
+        for c in range(0, points, 128):
+            acc = acc + jnp.maximum(sim[:cands, c:c + 128] - cover[:, c:c + 128], 0.0)
+        gains = jnp.where(lane == t, jnp.sum(acc, axis=1, keepdims=True), gains)
+        cover = jnp.maximum(cover, sim[cands + t:cands + t + 1, :])
+    gsend[...] = gains.reshape(n_mem, k1, 128)
+    gathers = [
+        pltpu.make_async_remote_copy(
+            src_ref=gsend.at[mem_peers[d]],
+            dst_ref=gbuf.at[mem],
+            send_sem=g_send.at[d - 1],
+            recv_sem=g_recv.at[d - 1],
+            device_id={"mem": mem_peers[d]},
+            device_id_type=MESH,
+        )
+        for d in mem_far
+    ]
+    for copy in gathers:
+        copy.start()
+    gbuf[mem] = gsend[mem]
 
     for copy in shares:
         copy.wait_recv()
@@ -178,10 +230,10 @@
             dst_ref=fin.at[:, my_cols],
             send_sem=fin_send.at[d - 1],
             recv_sem=fin_recv.at[d - 1],
-            device_id={"mem": mem_peer(d)},
-            device_id_type=MESH,
-        )
-        for d in range(1, n_mem)
+            device_id={"mem": mem_peers[d]},
+            device_id_type=MESH,
+        )
+        for d in mem_near
     ]
 
     def send_final():
@@ -191,53 +243,32 @@
 
     owner(send_final)
 
-    similar(2)
-    similar(3)
-
-    cover = jnp.max(sim[pl.ds(pl.multiple_of(mem * k1, k1), k1), :], axis=0, keepdims=True)
-    lane = lax.broadcasted_iota(jnp.int32, (cands, 128), 1)
-    gains = jnp.zeros((cands, 128), jnp.float32)
-    for t in range(k2):
-        acc = jnp.zeros((cands, 128), jnp.float32)
-        for c in range(0, points, 128):
-            acc = acc + jnp.maximum(sim[:cands, c:c + 128] - cover[:, c:c + 128], 0.0)
-        gains = jnp.where(lane == t, jnp.sum(acc, axis=1, keepdims=True), gains)
-        cover = jnp.maximum(cover, sim[cands + t:cands + t + 1, :])
-    gsend[...] = gains.reshape(n_mem, k1, 128)
-    gathers = [
-        pltpu.make_async_remote_copy(
-            src_ref=gsend.at[mem_peer(d)],
-            dst_ref=gbuf.at[mem],
-            send_sem=g_send.at[d - 1],
-            recv_sem=g_recv.at[d - 1],
-            device_id={"mem": mem_peer(d)},
-            device_id_type=MESH,
-        )
-        for d in range(1, n_mem)
-    ]
-    for copy in gathers:
-        copy.start()
-    gbuf[mem] = gsend[mem]
-
     if every:
-        for copy in finals:
+        def piece_of(place):
+            cols = pl.ds(pl.multiple_of(place * width, 128), width)
+            return lax.dot_general(
+                fin[:, cols], emb[:, :, cols].reshape(points, width), NT,
+                preferred_element_type=jnp.float32,
+            )
+
+        best = piece_of(mem)
+        for copy, d in zip(finals, mem_near):
             copy.wait_recv()
+            best = best + piece_of(mem_peers[d])
     else:
-        for d in range(1, n_mem):
-            pl.when(lax.rem(mem + n_mem - d, n_mem) < slices)(finals[d - 1].wait_recv)
-    final_rows = fin[...]
-    for i in range(4):
+        for d, copy in zip(mem_near, finals):
+            pl.when(peer_of(mem, n_mem, d) < slices)(copy.wait_recv)
         best = lax.dot_general(
-            final_rows, rows_of(i), NT, preferred_element_type=jnp.float32
-        )
-        cover_ref[:, i * tile:(i + 1) * tile] = jnp.max(best, axis=0, keepdims=True) * scale
+            fin[...], emb[...].reshape(points, depth), NT, preferred_element_type=jnp.float32
+        )
+    cover_ref[...] = jnp.max(best, axis=0, keepdims=True) * scale
 
     for copy in gathers:
         copy.wait_recv()
     total = jnp.sum(gbuf[...], axis=0) * (scale / points)
     gain_ref[...] = total[:, :k2]
 
-    for copy in parts + bulks + shares + gathers:
+    for copy in sum(bulks + relays, parts + shares + gathers):
         copy.wait_send()
 
     def sent_final():
@@ -272,7 +303,7 @@
             pltpu.SMEM(final_picks.shape, jnp.int32),
             pltpu.VMEM((k1, depth), half),
             pltpu.VMEM((n_mem, k1, width), half),
-            pltpu.VMEM((n_mem, k1, depth), half),
+            pltpu.VMEM((PIECES, n_mem, k1, depth // PIECES), half),
             pltpu.VMEM((n_grp, k3, width), half),
             pltpu.VMEM((k3, width), half),
             pltpu.VMEM((k3, depth), half),
@@ -281,7 +312,7 @@
             pltpu.VMEM((n_mem, k1, 128), jnp.float32),
             dma((LOADS,)), dma((3,)),
             dma((n_mem - 1,)), dma((n_mem - 1,)),
-            dma((n_mem - 1,)), dma((n_mem - 1,)),
+            dma((PIECES, n_mem - 1)), dma((PIECES, n_mem - 1)),
             dma((n_grp - 1,)), dma((n_grp - 1,)),
             dma((n_mem - 1,)), dma((n_mem - 1,)),
             dma((n_mem - 1,)), dma((n_mem - 1,)),

time: 23.6 us -> 22.6 us (0.958)
  Pallas kernels: 21.6 us -> 20.6 us
    pallas_call x1, Pallas kernels: 21.6 us -> 20.6 us  [per_device(): pl.pallas_call(functools.partial(kernel, n_grp, n_mem, slices), out_shape...]
where the time goes in v3:
time: 22.6 us; the launch traced here: 22.4 us
  Pallas kernels  20.6 us (91%)
  local copies, waits for them, and re-layouts  1.19 us (5%)
  between operations  0.64 us (3%)
    pallas_call x1, Pallas kernels, per_device(): pl.pallas_call(functools.partial(kernel, n_grp, n_mem, slices), out_shape...  20.6 us
    unnamed x2, local copies, waits for them, and re-layouts  1.19 us

profile of v3, /device:TPU:0, one launch (start us, length us, event | category | flops | bytes accessed | tf_op | source)
XLA Modules:
  0.0 22.4 jit_solution(14738106175360216744)
XLA Ops:
  0.6 20.6 %shard_map.59 = (f32[8,16]{1,0:T(8,128)S(1)}, f32[1,1024]{1,0:T(1,128)S(1)}) custom-call(bf16[64,16,4096]{2,1,0:T(8,128)(2,1)} %bitcast.5, s32[1,8]{1,0:T(1,128)} %local_hbm.1, s32[1,16]{1,0:T(1,128)} %second_hbm.1, s32[16]{0:T(128)} %final_hbm.1), custom_call_target="tpu_custom_call" | custom-call | tf_op jit(solution)/shard_map/pallas_call | solution.py:291
  21.2 0.6 %copy.8 = f32[16,8]{0,1:T(8,128)} copy(f32[16,8]{0,1:T(8,128)S(1)} %bitcast.4) | data formatting | bytes 1024
  21.8 0.6 %copy.9 = f32[1024]{0:T(1024)} copy(f32[1024]{0:T(1024)S(1)} %bitcast.3) | data formatting | bytes 8192

commit v4 on v3

--- a/solution.py
+++ b/solution.py
@@ -196,7 +196,38 @@
     cover = jnp.max(sim[pl.ds(pl.multiple_of(mem * k1, k1), k1), :], axis=0, keepdims=True)
     lane = lax.broadcasted_iota(jnp.int32, (cands, 128), 1)
     gains = jnp.zeros((cands, 128), jnp.float32)
-    for t in range(k2):
+    for t in range(k2 // 2):
+        acc = jnp.zeros((cands, 128), jnp.float32)
+        for c in range(0, points, 128):
+            acc = acc + jnp.maximum(sim[:cands, c:c + 128] - cover[:, c:c + 128], 0.0)
+        gains = jnp.where(lane == t, jnp.sum(acc, axis=1, keepdims=True), gains)
+        cover = jnp.maximum(cover, sim[cands + t:cands + t + 1, :])
+    for copy in shares:
+        copy.wait_recv()
+    total = zbuf[0].astype(jnp.float32)
+    for g in range(1, n_grp):
+        total = total + zbuf[g].astype(jnp.float32)
+    zsum[...] = total.astype(jnp.bfloat16)
+    finals = [
+        pltpu.make_async_remote_copy(
+            src_ref=zsum,
+            dst_ref=fin.at[:, my_cols],
+            send_sem=fin_send.at[d - 1],
+            recv_sem=fin_recv.at[d - 1],
+            device_id={"mem": mem_peers[d]},
+            device_id_type=MESH,
+        )
+        for d in mem_near
+    ]
+
+    def send_final():
+        for copy in finals:
+            copy.start()
+        fin[:, my_cols] = zsum[...]
+
+    owner(send_final)
+
+    for t in range(k2 // 2, k2):
         acc = jnp.zeros((cands, 128), jnp.float32)
         for c in range(0, points, 128):
             acc = acc + jnp.maximum(sim[:cands, c:c + 128] - cover[:, c:c + 128], 0.0)
@@ -217,31 +248,6 @@
     for copy in gathers:
         copy.start()
     gbuf[mem] = gsend[mem]
-
-    for copy in shares:
-        copy.wait_recv()
-    total = zbuf[0].astype(jnp.float32)
-    for g in range(1, n_grp):
-        total = total + zbuf[g].astype(jnp.float32)
-    zsum[...] = total.astype(jnp.bfloat16)
-    finals = [
-        pltpu.make_async_remote_copy(
-            src_ref=zsum,
-            dst_ref=fin.at[:, my_cols],
-            send_sem=fin_send.at[d - 1],
-            recv_sem=fin_recv.at[d - 1],
-            device_id={"mem": mem_peers[d]},
-            device_id_type=MESH,
-        )
-        for d in mem_near
-    ]
-
-    def send_final():
-        for copy in finals:
-            copy.start()
-        fin[:, my_cols] = zsum[...]
-
-    owner(send_final)
 
     if every:
         def piece_of(place):

time: 22.6 us -> 22.2 us (0.982)
  Pallas kernels: 20.6 us -> 20.2 us
    pallas_call x1, Pallas kernels: 20.6 us -> 20.2 us  [per_device(): pl.pallas_call(functools.partial(kernel, n_grp, n_mem, slices), out_shape...]
where the time goes in v4:
time: 22.2 us; the launch traced here: 22.1 us
  Pallas kernels  20.2 us (91%)
  local copies, waits for them, and re-layouts  1.19 us (5%)
  between operations  0.64 us (3%)
    pallas_call x1, Pallas kernels, per_device(): pl.pallas_call(functools.partial(kernel, n_grp, n_mem, slices), out_shape...  20.2 us
    unnamed x2, local copies, waits for them, and re-layouts  1.19 us

profile of v4, /device:TPU:0, one launch (start us, length us, event | category | flops | bytes accessed | tf_op | source)
XLA Modules:
  0.0 22.1 jit_solution(4631646258258945211)
XLA Ops:
  0.6 20.2 %shard_map.59 = (f32[8,16]{1,0:T(8,128)S(1)}, f32[1,1024]{1,0:T(1,128)S(1)}) custom-call(bf16[64,16,4096]{2,1,0:T(8,128)(2,1)} %bitcast.5, s32[1,8]{1,0:T(1,128)} %local_hbm.1, s32[1,16]{1,0:T(1,128)} %second_hbm.1, s32[16]{0:T(128)} %final_hbm.1), custom_call_target="tpu_custom_call" | custom-call | tf_op jit(solution)/shard_map/pallas_call | solution.py:297
  20.9 0.6 %copy.8 = f32[16,8]{0,1:T(8,128)} copy(f32[16,8]{0,1:T(8,128)S(1)} %bitcast.4) | data formatting | bytes 1024
  21.5 0.6 %copy.9 = f32[1024]{0:T(1024)} copy(f32[1024]{0:T(1024)S(1)} %bitcast.3) | data formatting | bytes 8192
